TPU v7x, 32 devices: a whole 2x2x4 slice. The times are simulated.
32 devices in a mesh: grp: 4 (over x, core), row: 4 (over z), col: 2 (over y).
Axes of the slice: x: 2, y: 2, z: 4, core: 2. Of those that a mesh axis runs over, the one named last changes fastest.
Arguments:
- cover: float32 [4, 12288, 4096], P('grp', 'row', 'col'), may hold values from -4 to 12, as said below
- prior: float32 [4096, 4096], P(('grp', 'row'), 'col'), may hold values from -0.5 to 2, as said below
Outputs:
- cover_out: float32 [4, 12288, 4096], P('grp', 'row', 'col')
- posterior: float32 [4096, 4096], P(('grp', 'row'), 'col')
Inputs may be any that keep to these rules, and one draw needn't show every extreme that they name: `cover`: the first three slots hold a symmetric positive definite matrix of order 12288 in the column-block order of the steps. `prior`: A symmetric positive definite matrix.
All inputs are finite; a program needn't handle non-finite values.
Results may differ from a plain program's by a relative error of at most 0.0001.
Values sent between devices are 32-bit elements; how exact they have to be, the bound alone decides.
No kernel may reach another device: no remote copies, remote signals or barrier semaphores. Data moves between devices by JAX's collectives and lax.ppermute only.
A program may use at most 192 MiB of HBM per device.

v0:
```python
import jax
import jax.numpy as jnp
from jax import lax
from jax.sharding import PartitionSpec as P

M = 12288
B = 256


precise = lax.Precision.HIGHEST


def broadcast(block, axis, source):
    block = jnp.where(lax.axis_index(axis) == source, block, jnp.zeros_like(block))
    return lax.psum(block, axis)


def advance(region, row_ids, block_ids, lower_rows, solved, panel, on_top):
    update = jnp.dot(lower_rows, solved, precision=precise, preferred_element_type=jnp.float32)
    to_right = block_ids > panel
    result = jnp.where((row_ids >= (panel + 1) * B) & to_right, region - update, region)
    own_column = (block_ids[:, :B] == panel) & (row_ids >= panel * B)
    result = jnp.concatenate(
        [jnp.where(own_column, lower_rows, result[:, :B]), result[:, B:]], axis=1
    )
    stripe = jnp.where(on_top & to_right, solved, result[panel * B : (panel + 1) * B])
    return jnp.concatenate([result[: panel * B], stripe, result[(panel + 1) * B :]], axis=0)


def local(cover, prior):
    local_block = cover[0]
    group_idx = lax.axis_index("grp")
    row_idx = lax.axis_index("row")
    col_idx = lax.axis_index("col")
    group_count = lax.axis_size("grp")
    row_count = lax.axis_size("row")
    col_count = lax.axis_size("col")
    local_rows, local_cols = local_block.shape
    prior_rows = prior.shape[0]
    row_ids = (row_idx * local_rows + jnp.arange(local_rows))[:, None]
    col_blocks = col_idx * (local_cols // B) + jnp.arange(local_cols) // B
    block_ids = jnp.where(
        group_idx < group_count - 1, (group_count - 1) * col_blocks + group_idx, M
    )[None, :]
    on_top = row_idx == 0
    first_col = (group_idx * row_count + row_idx) * prior_rows
    posterior = prior
    column_piece = local_block[:, :B]
    row_piece = local_block[0:B]
    panel_col = broadcast(column_piece, ("grp", "col"), 0 * col_count)
    packed = jnp.concatenate([panel_col[0:B], row_piece], axis=1)
    packed = broadcast(packed, "row", 0)
    factor = jnp.linalg.cholesky(packed[:, :B])
    lower_rows = lax.linalg.triangular_solve(
        factor, panel_col, left_side=False, lower=True, transpose_a=True
    )
    solved = lax.linalg.triangular_solve(factor, packed[:, B:], left_side=True, lower=True)
    local_block = advance(local_block, row_ids, block_ids, lower_rows, solved, 0, on_top)
    command_cols = broadcast(solved, "grp", group_count - 1)
    owner_idx = first_col // local_cols
    window = lax.dynamic_slice_in_dim(command_cols, first_col % local_cols, prior_rows, 1)
    command_rows = broadcast(window, "col", owner_idx)
    posterior = posterior - lax.dot_general(
        command_rows,
        command_cols,
        (((0,), (0,)), ((), ())),
        precision=precise,
        preferred_element_type=jnp.float32,
    )
    return (local_block[None], posterior)


def solution(mesh):
    return jax.shard_map(
        local,
        mesh=mesh,
        in_specs=(P("grp", "row", "col"), P(("grp", "row"), "col")),
        out_specs=(P("grp", "row", "col"), P(("grp", "row"), "col")),
        check_vma=False,
    )
```

profile of v0, /device:TPU:0, one launch (start us, length us, event | category | flops | bytes accessed | tf_op | source)
XLA Modules:
  0.0 432.4 jit_solution(17534666749890213730)
XLA Ops:
  7.2 24.7 %copy.4 = f32[1,3072,2048]{1,2,0:T(8,128)} copy(f32[1,3072,2048]{2,1,0:T(8,128)} %param.2) | data formatting | bytes 50331648 | tf_op args[0]
  31.9 3.9 slice_select_fusion.1
  35.8 0.0 all-reduce.8.cloned.1.call-start
  35.9 1.7 slice_bitcast_fusion
  37.6 70.4 %all-reduce.6.cloned.1.call-done = f32[3072,256]{0,1:T(8,128)} async-done(((f32[3072,256]{0,1:T(8,128)}), f32[3072,256]{0,1:T(8,128)}) %all-reduce.6.cloned.1.call-update) | async-done | bytes 3145744 | tf_op jit(solution)/shard_map/psum | solution.py:15
  108.0 1.0 slice.107
  109.0 1.6 maximum_select_fusion
  110.6 0.0 all-reduce.10.cloned.1.call-start
  110.8 94.6 %all-reduce.8.cloned.1.call-done = f32[256,2304]{0,1:T(8,128)} async-done(((f32[256,2304]{0,1:T(8,128)}), f32[256,2304]{0,1:T(8,128)}) %all-reduce.8.cloned.1.call-update) | async-done | bytes 2359312 | tf_op jit(solution)/shard_map/psum | solution.py:15
  205.4 1.0 slice.109
  206.4 0.1 copy.6
  206.5 1.0 fusion.7
  207.5 11.7 %cholesky.50 = f32[128,128]{1,0:T(8,128)S(1)} custom-call(f32[128,128]{1,0:T(8,128)S(1)} %cholesky.118), custom_call_target="Cholesky" | custom-call | tf_op jit(solution)/shard_map/jit(cholesky)/cholesky | solution.py:53
  219.3 9.8 %custom-call.16 = f32[1,128,128]{1,2,0:T(8,128)S(1)} custom-call(f32[1,128,128]{2,1,0:T(8,128)S(1)} %get-tuple-element.29), custom_call_target="InvertDiagBlocksLowerTriangular" | custom-call | tf_op jit(solution)/shard_map/jit(cholesky)/cholesky | solution.py:53
  229.1 0.2 fusion.8
  229.3 0.3 convolution_subtract_fusion.3
  229.6 11.7 %cholesky.105 = f32[128,128]{1,0:T(8,128)S(1)} custom-call(f32[128,128]{1,0:T(8,128)S(1)} %convolution_subtract_fusion.3), custom_call_target="Cholesky" | custom-call | tf_op jit(solution)/shard_map/jit(cholesky)/cholesky | solution.py:53
  241.3 0.1 copy.9
  241.4 0.1 copy.8
  241.5 0.1 copy.7
  241.6 0.7 compare_reduce_fusion.1
  243.7 0.1 triangular_solve.72
  243.7 4.2 while.1
  243.9 0.6 fusion.39
  244.5 1.3 dynamic-slice.7
  245.8 0.1 copy.17
  245.9 0.6 fusion.39
  246.5 1.3 dynamic-slice.7
  247.8 0.1 copy.17
  247.9 19.7 %custom-call.17 = f32[2,128,128]{1,2,0:T(8,128)S(1)} custom-call(f32[2,128,128]{2,1,0:T(8,128)S(1)} %get-tuple-element.9), custom_call_target="InvertDiagBlocksLowerTriangular" | custom-call | tf_op jit(solution)/shard_map/triangular_solve | solution.py:57
  267.6 2.3 fusion.5
  269.9 0.3 copy.11
  270.3 3.5 convolution_subtract_fusion.2
  273.7 1.0 fusion.12
  274.7 1.5 fusion.2
  276.3 1.6 convolution_subtract_fusion
  277.9 1.5 fusion.11
  279.4 27.7 %subtract_select_fusion = f32[3072,2048]{0,1:T(8,128)} fusion(pred[3072]{0:T(1024)(128)(4,1)S(1)} %get-tuple-element.30, pred[2048]{0:T(1024)(128)(4,1)S(1)} %get-tuple-element.32, f32[3072,128]{0,1:T(8,128)S(1)} %fusion.11, f32[3072,128]{0,1:T(8,128)S(1)} %fusion.2, f32[128,2048]{0,1:T(8,128)S(1)} %fusion.12, f32[128,2048]{0,1:T(8,128)S(1)} %copy.11, ...), kind=kOutput, calls=%fused_computation.2 | convolution fusion | flops 19347537920 | bytes 55579648 | tf_op jit(solution)/shard_map/dot_general | solution.py:19
  307.1 8.3 %slice.114 = f32[3072,1792]{0,1:T(8,128)S(1)} slice(f32[3072,2048]{0,1:T(8,128)} %subtract_select_fusion), slice={[0:3072], [256:2048]} | slice | bytes 44040192 | tf_op jit(solution)/shard_map/slice | solution.py:24
  315.4 4.9 %slice_select_fusion = f32[3072,256]{0,1:T(8,128)S(1)} fusion(f32[3072,2048]{0,1:T(8,128)} %subtract_select_fusion, f32[3072,128]{0,1:T(8,128)S(1)} %fusion.11, f32[3072,128]{0,1:T(8,128)S(1)} %fusion.2, pred[3072]{0:T(1024)(128)(4,1)S(1)} %get-tuple-element.31, pred[256]{0:T(512)(128)(4,1)S(1)} %compare_reduce_fusion), kind=kLoop, calls=%fused_computation.8 | loop fusion | flops 2359296 | bytes 9440512 | tf_op jit(solution)/shard_map/jit(_where)/select_n | solution.py:24
  320.4 0.4 copy-done.2
  320.7 3.0 fusion.4
  323.8 1.7 copy-done
  325.6 50.5 %all-reduce.10.cloned.1.call-done = f32[256,2048]{0,1:T(8,128)} async-done(((f32[256,2048]{0,1:T(8,128)}), f32[256,2048]{0,1:T(8,128)}) %all-reduce.10.cloned.1.call-update) | async-done | bytes 2097168 | tf_op jit(solution)/shard_map/psum | solution.py:15
  376.0 1.7 dynamic-slice_select_fusion
  377.7 18.3 %fusion.1 = f32[1,3072,2048]{1,2,0:T(8,128)} fusion(f32[3072,1792]{0,1:T(8,128)} %copy-done, f32[3072,256]{0,1:T(8,128)S(1)} %slice_select_fusion, f32[256,2048]{0,1:T(8,128)} %get-tuple-element.27), kind=kLoop, calls=%fused_computation.5 | loop fusion | flops 31457280 | bytes 52428800 | tf_op jit(solution)/shard_map/broadcast_in_dim | solution.py:70
  396.0 24.9 %copy.13 = f32[1,3072,2048]{2,1,0:T(8,128)} copy(f32[1,3072,2048]{1,2,0:T(8,128)} %fusion.1) | data formatting | bytes 50331648
  420.9 4.9 %convolution_subtract_fusion.1 = f32[256,2048]{1,0:T(8,128)} fusion(f32[256,2048]{1,0:T(8,128)} %param.3, f32[256,256]{0,1:T(8,128)} %all-reduce.12.cloned.1.call-done, f32[256,2048]{0,1:T(8,128)S(1)} %copy-done.4), kind=kOutput, calls=%fused_computation.11 | convolution fusion | flops 1611137024 | bytes 6553600 | tf_op jit(solution)/shard_map/dot_general | solution.py:63
  (33 shorter events, 0.4 us)
Async XLA Ops:
  7.2 100.9 %all-reduce.6.cloned.1.call-start = ((), (), s32[]{:S(2)}) async-start(), calls=%async_computation | async-start | bytes 6291456 | tf_op jit(solution)/shard_map/psum | solution.py:15
  35.8 169.6 %all-reduce.8.cloned.1.call-start = ((), (), s32[]{:S(2)}) async-start(), calls=%async_computation.1 | async-start | bytes 4718592 | tf_op jit(solution)/shard_map/psum | solution.py:15
  110.6 265.5 %all-reduce.10.cloned.1.call-start = ((), (), s32[]{:S(2)}) async-start(), calls=%async_computation.2 | async-start | bytes 4194304 | tf_op jit(solution)/shard_map/psum | solution.py:15
  270.2 9.2 %copy-start.1 = (f32[128,2048]{0,1:T(8,128)}, f32[128,2048]{0,1:T(8,128)S(1)}, u32[]{:S(2)}) copy-start(f32[128,2048]{0,1:T(8,128)S(1)} %copy.11) | copy-start | bytes 3145732
  270.3 4.5 %copy-start.3 = (f32[3072,256]{0,1:T(8,128)S(1)}, f32[3072,256]{0,1:T(8,128)}, u32[]{:S(2)}) copy-start(f32[3072,256]{0,1:T(8,128)} %all-reduce.6.cloned.1.call-done) | copy-start | bytes 9437188
  315.4 10.1 %copy-start = (f32[3072,1792]{0,1:T(8,128)}, f32[3072,1792]{0,1:T(8,128)S(1)}, u32[]{:S(2)}) copy-start(f32[3072,1792]{0,1:T(8,128)S(1)} %slice.114) | copy-start | bytes 66060292
  315.4 5.3 %copy-start.2 = (f32[128,2048]{0,1:T(8,128)S(1)}, f32[128,2048]{0,1:T(8,128)}, u32[]{:S(2)}) copy-start(f32[128,2048]{0,1:T(8,128)} %copy-done.1) | copy-start | bytes 3145732
  325.5 95.4 %all-reduce.12.cloned.1.call-start = ((), (), s32[]{:S(2)}) async-start(), calls=%async_computation.3 | async-start | bytes 524288 | tf_op jit(solution)/shard_map/psum | solution.py:15
  396.0 24.9 %copy-start.4 = (f32[256,2048]{0,1:T(8,128)S(1)}, f32[256,2048]{0,1:T(8,128)}, u32[]{:S(2)}) copy-start(f32[256,2048]{0,1:T(8,128)} %all-reduce.10.cloned.1.call-done) | copy-start | bytes 6291460
Sparse Core Ops, SparseCore 0:
  36.0 72.0 all-reduce.5
  110.7 94.6 all-reduce.7
  325.6 50.3 all-reduce.9
  378.7 23.3 all-reduce.11
where the time goes:
time: 433 us; the launch traced here: 432 us
  waiting for transfers between devices  216 us (50%)
  other arithmetic  88.2 us (20%)
  local copies, waits for them, and re-layouts  68.4 us (16%)
  matrix products  44.5 us (10%)
  between operations  15.3 us (4%)
    psum x4, waiting for transfers between devices, broadcast(): return lax.psum(block, axis)  215 us
    unnamed x12, local copies, waits for them, and re-layouts  51.6 us
    another operation x6, other arithmetic, local(): factor = jnp.linalg.cholesky(packed[:, :B])  34 us
    dot_general x1, matrix products, advance(): jnp.dot(lower_rows, solved, precision=precise, preferred_element_type=jnp...  27.7 us
    another operation x3, other arithmetic, local(): lax.linalg.triangular_solve(factor, packed[:, B:], left_side=True, lower=...  19.7 us
    broadcast_in_dim x1, other arithmetic, local(): return (local_block[None], posterior)  18.3 us
    select_n x4, other arithmetic, broadcast(): jnp.where(lax.axis_index(axis) == source, block, jnp.zeros_like(block))  10.2 us
  transfers between devices with their start and end apart: 4, of which 3 were waited for; matrix products, arithmetic and copies ran while one was open for 10% of the time, Pallas kernels for 0%

commit v1 on v0

v1 whole, which is shorter than its diff:
```python
import functools

import jax
import jax.numpy as jnp
from jax import lax
from jax.experimental import pallas as pl
from jax.experimental.pallas import tpu as pltpu
from jax.sharding import PartitionSpec as P


B = 256
NB = 64
AXES = ("grp", "row", "col")


def dot(a, b, dims=(((1,), (0,)), ((), ()))):
    return lax.dot_general(
        a, b, dims, precision=lax.Precision.HIGHEST, preferred_element_type=jnp.float32
    )


def split(a):
    high = a.astype(jnp.bfloat16)
    return high, (a - high.astype(jnp.float32)).astype(jnp.bfloat16)


def dot3(a, b, dims=(((1,), (0,)), ((), ()))):
    a_high, a_low = split(a)
    b_high, b_low = split(b)
    f = functools.partial(
        lax.dot_general, dimension_numbers=dims, preferred_element_type=jnp.float32
    )
    return f(a_high, b_high) + (f(a_high, b_low) + f(a_low, b_high))


def eliminate(tile):
    sub = lax.broadcasted_iota(jnp.int32, (8, 128), 0)
    count = NB // 8
    x = [tile[8 * v : 8 * v + 8, :] for v in range(count)]
    full = lambda a: jnp.broadcast_to(a, (8, 128))
    for s in range(count):
        bc = {
            v: [full(x[v][:, 8 * s + k : 8 * s + k + 1]) for k in range(8)]
            for v in range(s, count)
        }
        e = [[full(bc[s][k][i : i + 1, :]) for k in range(i + 1)] for i in range(8)]
        r = [full(x[s][i : i + 1, :]) for i in range(8)]
        inv, m = [], {}
        for j in range(8):
            inv.append(1.0 / e[j][j])
            for i in range(j + 1, 8):
                m[i, j] = e[i][j] * inv[j]
            for i in range(j + 1, 8):
                for l in range(j + 1, i + 1):
                    e[i][l] = e[i][l] - m[i, j] * e[l][j]
                r[i] = r[i] - m[i, j] * r[j]
        if s + 1 < count:
            z = [None] * 8
            for i in range(7, -1, -1):
                t = r[i] * inv[i]
                for k in range(7, i, -1):
                    t = t - m[k, i] * z[k]
                z[i] = t
            for v in range(s + 1, count):
                t0 = bc[v][0] * z[0]
                t1 = bc[v][1] * z[1]
                for k in range(2, 8, 2):
                    t0 = t0 + bc[v][k] * z[k]
                    t1 = t1 + bc[v][k + 1] * z[k + 1]
                x[v] = x[v] - (t0 + t1)
        rows, d = r[0], e[0][0]
        for i in range(1, 8):
            rows = jnp.where(sub == i, r[i], rows)
            d = jnp.where(sub == i, e[i][i], d)
        x[s] = rows * lax.rsqrt(d)
    return jnp.concatenate(x, axis=0)


def factor_kernel(d_ref, g_ref, x_ref):
    n = d_ref.shape[0]
    eye = lambda m: (
        lax.broadcasted_iota(jnp.int32, (m, m), 0) == lax.broadcasted_iota(jnp.int32, (m, m), 1)
    ).astype(jnp.float32)
    x_ref[:, :n] = d_ref[...]
    x_ref[:, n:] = eye(n)
    for lo in range(0, n, NB):
        hi = lo + NB
        tile = jnp.concatenate([x_ref[lo:hi, lo:hi], eye(NB)], axis=1)
        inverse = eliminate(tile)[:, NB:]
        u = dot(inverse, x_ref[lo:hi, :])
        x_ref[lo:hi, :] = u
        if hi < n:
            x_ref[hi:, :] = x_ref[hi:, :] - dot(u[:, hi:n], u, (((0,), (0,)), ((), ())))
    g_ref[...] = x_ref[:, n:]


def inverse_factor(d):
    n = d.shape[0]
    return pl.pallas_call(
        factor_kernel,
        out_shape=jax.ShapeDtypeStruct((n, n), jnp.float32),
        scratch_shapes=[pltpu.VMEM((n, 2 * n), jnp.float32)],
        compiler_params=pltpu.CompilerParams(vmem_limit_bytes=8 << 20),
        cost_estimate=pl.CostEstimate(flops=4_000_000_000, bytes_accessed=1 << 20, transcendentals=0),
        name="factor",
    )(d)


def copy_in(pieces, sems):
    made = [pltpu.make_async_copy(s, d, sems.at[i]) for i, (_, s, d) in enumerate(pieces)]
    for (cond, _, _), c in zip(pieces, made):
        pl.when(cond)(c.start)

    def wait():
        for (cond, _, _), c in zip(pieces, made):
            pl.when(cond)(c.wait)

    return wait


def update_kernel(plan, n_p, n_r, a_ref, g_ref, whole_ref, *refs):
    p_refs = refs[:n_p]
    r_refs = refs[n_p : n_p + n_r]
    out_ref, p_buf, r_buf, w_buf, w3_buf, p_sems, r_sems = refs[n_p + n_r :]
    step = pl.program_id(0)
    group, row, col = (lax.axis_index(a) for a in AXES)
    tile = a_ref.shape[0]

    @pl.when(step == 0)
    def _():
        p_plan, r_plan = plan(group, row, col, whole_ref, p_refs, r_refs, p_buf, r_buf)
        wait_r = copy_in(r_plan, r_sems)
        wait_p = copy_in(p_plan, p_sems)
        wait_r()
        w = dot3(g_ref[...], r_buf[...])
        w_buf[...] = w
        high, low = split(w)
        w3_buf[0:B, :] = high
        w3_buf[B : 2 * B, :] = low
        w3_buf[2 * B :, :] = high
        wait_p()

    lower = dot3(p_buf[pl.ds(step * tile, tile), :], g_ref[...], (((1,), (1,)), ((), ())))
    high, low = split(lower)
    parts = jnp.concatenate([high, high, low], axis=1)
    cols = a_ref.shape[1]
    step_cols = min(512, cols)
    for c in range(0, cols, step_cols):
        out_ref[:, c : c + step_cols] = a_ref[:, c : c + step_cols] - jnp.dot(
            parts, w3_buf[:, c : c + step_cols], preferred_element_type=jnp.float32
        )

    @pl.when((row == 0) & (step * tile < B))
    def _():
        out_ref[0:B, :] = w_buf[...]

    @pl.when((group == 0) & (col == 0))
    def _():
        out_ref[:, 0:B] = lower


def update(plan, sizes, a, g, p_list, r_list):
    rows, cols = a.shape
    tile = 2 * B if rows % (2 * B) == 0 else B
    any_spec = pl.BlockSpec(memory_space=pl.ANY)
    n_p, n_r = len(p_list), len(r_list)
    n_pp, n_rp = sizes
    return pl.pallas_call(
        functools.partial(update_kernel, plan, n_p, n_r),
        grid=(rows // tile,),
        in_specs=[
            pl.BlockSpec((tile, cols), lambda i: (i, 0)),
            pl.BlockSpec((B, B), lambda i: (0, 0)),
            any_spec,
        ]
        + [any_spec] * (n_p + n_r),
        out_specs=pl.BlockSpec((tile, cols), lambda i: (i, 0)),
        out_shape=jax.ShapeDtypeStruct((rows, cols), jnp.float32),
        scratch_shapes=[
            pltpu.VMEM((rows, B), jnp.float32),
            pltpu.VMEM((B, cols), jnp.float32),
            pltpu.VMEM((B, cols), jnp.float32),
            pltpu.VMEM((3 * B, cols), jnp.bfloat16),
            pltpu.SemaphoreType.DMA((n_pp,)),
            pltpu.SemaphoreType.DMA((n_rp,)),
        ],
        compiler_params=pltpu.CompilerParams(vmem_limit_bytes=62 << 20),
        cost_estimate=pl.CostEstimate(
            flops=6 * rows * cols * B, bytes_accessed=8 * rows * cols, transcendentals=0
        ),
        name="update",
    )(a, g, a, *p_list, *r_list)


def posterior_kernel(prior_ref, g_ref, win_ref, x_ref, out_ref):
    g = g_ref[...]
    y = dot3(g, x_ref[...])
    y_win = dot3(g, win_ref[...])
    out_ref[...] = prior_ref[...] - dot3(y_win, y, (((0,), (0,)), ((), ())))


def posterior_update(prior, g, window, x):
    return pl.pallas_call(
        posterior_kernel,
        out_shape=jax.ShapeDtypeStruct(prior.shape, jnp.float32),
        compiler_params=pltpu.CompilerParams(vmem_limit_bytes=32 << 20),
        cost_estimate=pl.CostEstimate(
            flops=6 * prior.shape[0] * prior.shape[1] * B,
            bytes_accessed=6 * prior.size,
            transcendentals=0,
        ),
        name="posterior",
    )(prior, g, window, x)


def panel(cover, prior):
    a = cover[0]
    group, row, col = (lax.axis_index(x) for x in AXES)
    gn, rn, cn = (lax.axis_size(x) for x in AXES)
    rows, cols = a.shape
    core = group % 2
    ident = lambda g, r, c: (g * rn + r) * cn + c

    def send(x, pairs):
        return lax.ppermute(x, AXES, [(ident(*s), ident(*d)) for s, d in pairs])

    all_r, all_c = range(rn), range(cn)
    mid = rn // 2
    others = [r for r in range(1, rn) if r != mid]

    steps = []
    d = 1
    while d < cn:
        steps.append(d)
        d *= 2
    along_x = [((0, c), (x, c)) for c in all_c for x in range(1, gn // 2)]

    def tree(c_first):
        out = []
        for d in steps:
            xs = [0] if c_first else range(gn // 2)
            out.append([((x, c), (x, c + d)) for x in xs for c in range(d)])
        if c_first:
            return out + [along_x]
        return [[p for p in along_x if p[0][1] == 0]] + out

    def on_cores(first, second):
        return [
            ((2 * x + k, r, c), (2 * x_ + k, r, c_))
            for k, pairs in ((0, first), (1, second))
            for (x, c), (x_, c_) in pairs
            for r in all_r
        ]

    diag = jnp.where((group == 0) & (row == 0) & (col == 0), a[0:B, 0:B], 0.0)
    diag = diag + sum(send(diag, [((0, 0, 0), (0, r, 0))]) for r in range(1, rn))
    diag = diag + send(diag, [((0, r, 0), (1, r, 0)) for r in all_r])
    if (gn, cn) == (4, 2):
        hops = [
            [((0, 0), (0, 1)), ((1, 0), (3, 0))],
            [((3, 0), (2, 0)), ((0, 1), (2, 1))],
            [((0, 1), (1, 1)), ((2, 1), (3, 1))],
        ]
        hops = [[((p, r, c), (q, r, e)) for (p, c), (q, e) in h for r in all_r] for h in hops]
    else:
        hops = [on_cores(*pair) for pair in zip(tree(True), tree(False))]
    for pairs in hops:
        diag = diag + send(diag, pairs)
    g = inverse_factor(diag)

    half = rows // 2
    top, bottom = a[:half, 0:B], a[half:, 0:B]
    firsts, seconds = tree(False), tree(True)
    source = lambda p: p[0] == (0, 0)
    part = send(bottom, [((0, r, 0), (1, r, 0)) for r in all_r])
    part = part + send(top, on_cores(filter(source, firsts[0]), []))
    part = part + send(
        bottom, [((0, r, 0), (2 * x + 1, r, c)) for _, (x, c) in seconds[0] for r in all_r]
    )
    part = jnp.where((group == 0) & (col == 0), top, part)
    for pair in zip(firsts[1:], seconds[1:]):
        part = part + send(part, on_cores(*pair))
    rest = send(part, [((g_, r, c), (g_ ^ 1, r, c)) for g_ in range(gn) for r in all_r for c in all_c])

    last = gn - 1
    units = cols // 128
    u = -(-units * 5 // 16)
    widths = [128 * u, 128 * max(1, units * 3 // 8)]
    widths.append(cols - sum(widths))
    starts = [0, widths[0], widths[0] + widths[1]]
    each = [(g_, c) for g_ in range(gn) for c in all_c]
    r_list, r_keys, xs = [], [], []
    own = lax.optimization_barrier([a[0:B, s : s + w] for s, w in zip(starts, widths)])
    mids = [send(p, [((g_, 0, c), (g_, mid, c)) for g_, c in each]) for p in own]
    for s, w, p, m in zip(starts, widths, own, mids):
        r_list.append(m)
        r_keys.append((s, w, mid))
        got = m
        for r in others:
            o = send(m, [((g_, mid, c), (g_, r, c)) for g_, c in each])
            r_list.append(o)
            r_keys.append((s, w, r))
            got = got + o
        got = jnp.where(group == last, jnp.where(row == 0, p, got), 0.0)
        for to in range(1, last, 2):
            got = got + send(got, [((last, r, c), (to, r, c)) for r in all_r for c in all_c])
        xs.append(got)

    def plan(group, row, col, whole, p_refs, r_refs, p_buf, r_buf):
        even = lax.rem(group, 2) == 0
        top, bottom = p_buf.at[:half, :], p_buf.at[half:, :]
        p_plan = [
            (even, p_refs[0], top),
            (even, p_refs[1], bottom),
            (~even, p_refs[1], top),
            (~even, p_refs[0], bottom),
        ]
        r_plan = [(row == 0, whole.at[0:B, :], r_buf)]
        for (s, w, r), ref in zip(r_keys, r_refs):
            r_plan.append((row == r, ref, r_buf.at[:, s : s + w]))
        return p_plan, r_plan

    block = update(plan, (4, 1 + len(r_keys)), a, g, [part, rest], r_list)

    width = prior.shape[0]
    x = jnp.concatenate(xs, axis=1)
    down = [((g_, r, c), (g_ - 1, r, c)) for g_ in range(1, gn, 2) for r in all_r for c in all_c]
    x_over = send(x, down)
    owner = lambda g_, r: (g_ * rn + r) * width // cols

    def window_of(shift):
        first = ((group - shift) * rn + row) * width
        piece = lax.dynamic_slice_in_dim(x, lax.rem(first + gn * cols, cols), width, 1)
        got = [
            send(
                piece,
                [
                    ((g_, r, owner(g_ - shift, r)), (g_, r, (owner(g_ - shift, r) + d) % cn))
                    for g_ in range(1, gn, 2)
                    for r in all_r
                ],
            )
            for d in range(1, cn)
        ]
        return jnp.where(first // cols == col, piece, sum(got))

    window = window_of(0)
    window_over = send(window_of(1), down)
    window = jnp.where(core == 1, window, window_over)
    x = jnp.where(core == 1, x, x_over)
    return block[None], posterior_update(prior, g, window, x)


def solution(mesh):
    return jax.shard_map(
        panel,
        mesh=mesh,
        in_specs=(P("grp", "row", "col"), P(("grp", "row"), "col")),
        out_specs=(P("grp", "row", "col"), P(("grp", "row"), "col")),
        check_vma=False,
    )
```

time: 433 us -> 200 us (0.46)
  the two profiles are of different devices: /device:TPU:0 before, /device:TPU:14 now
where the time goes in v1:
time: 200 us; the launch traced here: 199 us
  waiting for transfers between devices  95.4 us (48%)
  Pallas kernels  42 us (21%)
  starting transfers between devices  32.4 us (16%)
  other arithmetic  18.4 us (9%)
  local copies, waits for them, and re-layouts  9.08 us (5%)
    ppermute x28, waiting for transfers between devices, send(): return lax.ppermute(x, AXES, [(ident(*s), ident(*d)) for s, d in pairs])  95.4 us
    ppermute x28, starting transfers between devices, send(): return lax.ppermute(x, AXES, [(ident(*s), ident(*d)) for s, d in pairs])  32.4 us
    pallas_call x1, Pallas kernels, update(): pl.pallas_call(functools.partial(update_kernel, plan, n_p, n_r), grid=(ro...  27 us
    pallas_call x1, Pallas kernels, inverse_factor(): pl.pallas_call(factor_kernel, out_shape=jax.ShapeDtypeStruct((n, n), jnp....  11.2 us
  transfers between devices with their start and end apart: 28, of which 4 were waited for; matrix products, arithmetic and copies ran while one was open for 12% of the time, Pallas kernels for 8%

profile of v1, /device:TPU:14, one launch (start us, length us, event | category | flops | bytes accessed | tf_op | source)
XLA Modules:
  0.0 198.7 jit_solution(13942553619841189461)
XLA Ops:
  0.6 1.2 slice.28
  1.8 2.2 %fusion = (f32[256,640]{1,0:T(8,128)S(1)}, f32[256,640]{1,0:T(8,128)}) fusion(f32[3072,2048]{1,0:T(8,128)} %bitcast.3), kind=kLoop, calls=%fused_computation.12 | loop fusion | bytes 2621440 | tf_op jit(solution)/shard_map/slice | solution.py:293
  4.0 0.7 collective-permute-start.15
  4.7 0.7 collective-permute-start.12
  5.4 1.5 collective-permute-start.18
  7.0 0.7 collective-permute-start.14
  7.7 1.3 collective-permute-start.13
  9.0 0.7 collective-permute-start.17
  9.7 1.3 collective-permute-start.16
  11.0 3.8 %fusion.1 = (f32[1536,256]{1,0:T(8,128)}, f32[1536,256]{1,0:T(8,128)}) fusion(f32[3072,2048]{1,0:T(8,128)} %bitcast.4), kind=kLoop, calls=%fused_computation.13 | loop fusion | bytes 6291456 | tf_op jit(solution)/shard_map/slice | solution.py:272
  14.8 1.9 collective-permute-start.8
  16.7 1.8 collective-permute-start.9
  18.5 42.5 %collective-permute-done.13.refs_3_ = f32[256,640]{1,0:T(8,128)S(1)} collective-permute-done((f32[256,640]{1,0:T(8,128)S(1)}, f32[256,640]{1,0:T(8,128)S(1)}, u32[]{:S(2)}, u32[]{:S(2)}) %collective-permute-start.13) | collective-permute-done | bytes 655392 | tf_op jit(solution)/shard_map/ppermute | solution.py:225
  61.0 1.8 collective-permute-start.7
  62.9 1.5 collective-permute-start.20
  64.4 10.7 %collective-permute-done.16.refs_6_ = f32[256,768]{1,0:T(8,128)S(1)} collective-permute-done((f32[256,768]{1,0:T(8,128)S(1)}, f32[256,768]{1,0:T(8,128)S(1)}, u32[]{:S(2)}, u32[]{:S(2)}) %collective-permute-start.16) | collective-permute-done | bytes 786464 | tf_op jit(solution)/shard_map/ppermute | solution.py:225
  75.0 1.3 collective-permute-start.19
  76.3 1.0 slice_select_fusion
  77.3 1.6 select_select_fusion.2
  79.2 0.7 collective-permute-start.2
  79.9 12.1 %collective-permute-done.19.refs_9_ = f32[256,640]{1,0:T(8,128)} collective-permute-done((f32[256,640]{1,0:T(8,128)}, f32[256,640]{1,0:T(8,128)}, u32[]{:S(2)}, u32[]{:S(2)}) %collective-permute-start.19) | collective-permute-done | bytes 655392 | tf_op jit(solution)/shard_map/ppermute | solution.py:225
  92.0 0.7 collective-permute-start.22
  92.7 1.6 select_select_fusion.1
  94.3 0.7 collective-permute-start.1
  95.0 0.7 collective-permute-start.21
  95.7 0.7 collective-permute-start.23
  96.4 3.2 %add_select_fusion = f32[1536,256]{1,0:T(8,128)S(1)} fusion(f32[1536,256]{1,0:T(8,128)} %collective-permute-done.9, f32[1536,256]{1,0:T(8,128)} %collective-permute-done.7, f32[1536,256]{1,0:T(8,128)} %collective-permute-done.8, pred[]{:T(512)S(6)} %and.30, f32[3072,2048]{1,0:T(8,128)} %bitcast.6), kind=kLoop, calls=%fused_computation.1 | loop fusion | flops 1179648 | bytes 7864321 | tf_op jit(solution)/shard_map/jit(_where)/select_n | solution.py:280
  99.7 0.7 collective-permute-start
  100.5 1.3 collective-permute-start.10
  101.9 1.6 pad_maximum_fusion
  103.5 1.3 collective-permute-start.27
  104.8 1.0 add_add_fusion
  105.9 0.7 collective-permute-start.3
  107.4 1.3 collective-permute-start.5
  108.7 30.1 %collective-permute-done.5 = f32[256,256]{1,0:T(8,128)} collective-permute-done((f32[256,256]{1,0:T(8,128)S(1)}, f32[256,256]{1,0:T(8,128)}, u32[]{:S(2)}, u32[]{:S(2)}) %collective-permute-start.5) | collective-permute-done | bytes 262176 | tf_op jit(solution)/shard_map/ppermute | solution.py:225
  138.7 1.0 add.87
  139.7 2.0 %collective-permute-start.6 = (f32[256,256]{1,0:T(8,128)S(1)}, f32[256,256]{1,0:T(8,128)}, u32[]{:S(2)}, u32[]{:S(2)}) collective-permute-start(f32[256,256]{1,0:T(8,128)S(1)} %add.87), channel_id=1, source_target_pairs={{1,9},{3,11},{5,13},{7,15},{17,25},{19,27},{21,29},{23,31}} | collective-permute-start | bytes 786440 | tf_op jit(solution)/shard_map/ppermute | solution.py:225
  141.7 1.8 constant_dynamic-slice_fusion.1
  143.5 1.4 collective-permute-start.25
  144.9 2.8 %add.91.refs_0_ = f32[1536,256]{1,0:T(8,128)} add(f32[1536,256]{1,0:T(8,128)S(1)} %add_select_fusion, f32[1536,256]{1,0:T(8,128)} %collective-permute-done.10) | non-fusion elementwise | flops 393216 | bytes 4718592 | tf_op jit(solution)/shard_map/add | solution.py:282
  147.6 2.2 %collective-permute-start.11 = (f32[1536,256]{1,0:T(8,128)}, f32[1536,256]{1,0:T(8,128)}, u32[]{:S(2)}, u32[]{:S(2)}) collective-permute-start(f32[1536,256]{1,0:T(8,128)} %add.91.refs_0_), channel_id=1, source_target_pairs={{0,8},{1,9},{2,10},{3,11},{4,12},{5,13},{6,14},{7,15},{8,0},{9,1},... | collective-permute-start | bytes 4718600 | tf_op jit(solution)/shard_map/ppermute | solution.py:225
  149.8 1.0 add.88.d_ref
  151.5 1.0 broadcast_select_fusion.1
  152.5 1.6 collective-permute-start.26
  154.1 11.2 %factor.1.g_ref = f32[256,256]{1,0:T(8,128)S(1)} custom-call(f32[256,256]{1,0:T(8,128)S(1)} %add.88.d_ref), custom_call_target="tpu_custom_call" | custom-call | flops 4000000000 | bytes 1048576 | tf_op jit(solution)/shard_map/factor/pallas_call | solution.py:99
  165.5 2.1 %broadcast_select_fusion.x_ref = f32[256,2048]{1,0:T(8,128)S(1)} fusion(f32[256,2048]{1,0:T(8,128)} %collective-permute-done.27, pred[]{:T(512)S(6)} %eq.34, f32[256,640]{1,0:T(8,128)S(1)} %copy-done.3, f32[256,768]{1,0:T(8,128)S(1)} %add.99, f32[256,640]{1,0:T(8,128)S(1)} %add.96), kind=kLoop, calls=%fused_computation.2 | loop fusion | flops 1572864 | bytes 6291457 | tf_op jit(solution)/shard_map/jit(_where)/select_n | solution.py:350
  167.7 3.8 %posterior.1 = f32[256,2048]{1,0:T(8,128)} custom-call(f32[256,2048]{1,0:T(8,128)S(1)} %copy-done, f32[256,256]{1,0:T(8,128)S(1)} %factor.1.g_ref, f32[256,256]{1,0:T(8,128)S(1)} %select_select_fusion.3.win_ref, f32[256,2048]{1,0:T(8,128)S(1)} %broadcast_select_fusion.x_ref), custom_call_target="tpu_custom_call" | custom-call | flops 805306368 | bytes 3145728 | tf_op jit(solution)/shard_map/posterior/pallas_call | solution.py:203
  171.5 27.0 %update.1 = f32[3072,2048]{1,0:T(8,128)} custom-call(f32[3072,2048]{1,0:T(8,128)} %bitcast.8, f32[256,256]{1,0:T(8,128)} %copy-done.1, f32[3072,2048]{1,0:T(8,128)} %bitcast.9, f32[1536,256]{1,0:T(8,128)} %add.91.refs_0_, f32[1536,256]{1,0:T(8,128)} %collective-permute-done.11.refs_1_, f32[256,640]{1,0:T(8,128)} %copy-done.9, f32[256,640]{1,0:T(8,128)} %copy-done.11, ...), custom_call_target="tpu_custom_call" | custom-call | flops 9663676416 | bytes 50331648 | tf_op jit(solution)/shard_map/update/pallas_call | solution.py:168
  (57 shorter events, 2.1 us)
Async XLA Ops:
  4.0 10.7 %copy-start.7 = (f32[256,640]{1,0:T(8,128)}, f32[256,640]{1,0:T(8,128)S(1)}, u32[]{:S(2)}) copy-start(f32[256,640]{1,0:T(8,128)S(1)} %get-tuple-element.7) | copy-start | bytes 1966084
  4.0 4.9 %collective-permute-start.15 = (f32[256,768]{1,0:T(8,128)S(1)}, f32[256,768]{1,0:T(8,128)S(1)}, u32[]{:S(2)}, u32[]{:S(2)}) collective-permute-start(f32[256,768]{1,0:T(8,128)S(1)} %slice.28), channel_id=1, source_target_pairs={{0,4},{1,5},{8,12},{9,13},{16,20},{17,21},{24,28},{25,29}} | collective-permute-start | bytes 2359304 | tf_op jit(solution)/shard_map/ppermute | solution.py:225
  4.7 2.2 %collective-permute-start.12 = (f32[256,640]{1,0:T(8,128)}, f32[256,640]{1,0:T(8,128)S(1)}, u32[]{:S(2)}, u32[]{:S(2)}) collective-permute-start(f32[256,640]{1,0:T(8,128)} %get-tuple-element.5), channel_id=1, source_target_pairs={{0,4},{1,5},{8,12},{9,13},{16,20},{17,21},{24,28},{25,29}} | collective-permute-start | bytes 1966088 | tf_op jit(solution)/shard_map/ppermute | solution.py:225
  5.4 9.3 %collective-permute-start.18 = (f32[256,640]{1,0:T(8,128)S(1)}, f32[256,640]{1,0:T(8,128)}, u32[]{:S(2)}, u32[]{:S(2)}) collective-permute-start(f32[256,640]{1,0:T(8,128)S(1)} %get-tuple-element.7), channel_id=1, source_target_pairs={{0,4},{1,5},{8,12},{9,13},{16,20},{17,21},{24,28},{25,29}} | collective-permute-start | bytes 1966088 | tf_op jit(solution)/shard_map/ppermute | solution.py:225
  7.0 7.8 %copy-start.9 = (f32[256,640]{1,0:T(8,128)}, f32[256,640]{1,0:T(8,128)S(1)}, u32[]{:S(2)}) copy-start(f32[256,640]{1,0:T(8,128)S(1)} %collective-permute-done.12.refs_2_) | copy-start | bytes 1966084
  7.0 9.7 %collective-permute-start.14 = (f32[256,640]{1,0:T(8,128)S(1)}, f32[256,640]{1,0:T(8,128)S(1)}, u32[]{:S(2)}, u32[]{:S(2)}) collective-permute-start(f32[256,640]{1,0:T(8,128)S(1)} %collective-permute-done.12.refs_2_), channel_id=1, source_target_pairs={{4,6},{5,7},{12,14},{13,15},{20,22},{21,23},{28,30},{29,31}} | collective-permute-start | bytes 1966088 | tf_op jit(solution)/shard_map/ppermute | solution.py:225
  7.7 53.4 %collective-permute-start.13 = (f32[256,640]{1,0:T(8,128)S(1)}, f32[256,640]{1,0:T(8,128)S(1)}, u32[]{:S(2)}, u32[]{:S(2)}) collective-permute-start(f32[256,640]{1,0:T(8,128)S(1)} %collective-permute-done.12.refs_2_), channel_id=1, source_target_pairs={{4,2},{5,3},{12,10},{13,11},{20,18},{21,19},{28,26},{29,27}} | collective-permute-start | bytes 1966088 | tf_op jit(solution)/shard_map/ppermute | solution.py:225
  9.0 70.0 %copy-start.4 = (f32[256,768]{1,0:T(8,128)}, f32[256,768]{1,0:T(8,128)S(1)}, u32[]{:S(2)}) copy-start(f32[256,768]{1,0:T(8,128)S(1)} %collective-permute-done.15.refs_5_) | copy-start | bytes 2359300
  9.0 53.9 %collective-permute-start.17 = (f32[256,768]{1,0:T(8,128)S(1)}, f32[256,768]{1,0:T(8,128)S(1)}, u32[]{:S(2)}, u32[]{:S(2)}) collective-permute-start(f32[256,768]{1,0:T(8,128)S(1)} %collective-permute-done.15.refs_5_), channel_id=1, source_target_pairs={{4,6},{5,7},{12,14},{13,15},{20,22},{21,23},{28,30},{29,31}} | collective-permute-start | bytes 2359304 | tf_op jit(solution)/shard_map/ppermute | solution.py:225
  9.7 65.3 %collective-permute-start.16 = (f32[256,768]{1,0:T(8,128)S(1)}, f32[256,768]{1,0:T(8,128)S(1)}, u32[]{:S(2)}, u32[]{:S(2)}) collective-permute-start(f32[256,768]{1,0:T(8,128)S(1)} %collective-permute-done.15.refs_5_), channel_id=1, source_target_pairs={{4,2},{5,3},{12,10},{13,11},{20,18},{21,19},{28,26},{29,27}} | collective-permute-start | bytes 2359304 | tf_op jit(solution)/shard_map/ppermute | solution.py:225
  14.8 79.5 %collective-permute-start.8 = (f32[1536,256]{1,0:T(8,128)}, f32[1536,256]{1,0:T(8,128)}, u32[]{:S(2)}, u32[]{:S(2)}) collective-permute-start(f32[1536,256]{1,0:T(8,128)} %get-tuple-element.10), channel_id=1, source_target_pairs={{0,16},{2,18},{4,20},{6,22}} | collective-permute-start | bytes 4718600 | tf_op jit(solution)/shard_map/ppermute | solution.py:225
  16.7 44.3 %copy-start.10 = (f32[256,640]{1,0:T(8,128)}, f32[256,640]{1,0:T(8,128)S(1)}, u32[]{:S(2)}) copy-start(f32[256,640]{1,0:T(8,128)S(1)} %collective-permute-done.14.refs_4_) | copy-start | bytes 1966084
  16.7 78.3 %collective-permute-start.9 = (f32[1536,256]{1,0:T(8,128)}, f32[1536,256]{1,0:T(8,128)}, u32[]{:S(2)}, u32[]{:S(2)}) collective-permute-start(f32[1536,256]{1,0:T(8,128)} %get-tuple-element.11), channel_id=1, source_target_pairs={{0,9},{2,11},{4,13},{6,15}} | collective-permute-start | bytes 4718600 | tf_op jit(solution)/shard_map/ppermute | solution.py:225
  61.0 1.8 copy-start.11
  61.0 34.7 %collective-permute-start.7 = (f32[1536,256]{1,0:T(8,128)}, f32[1536,256]{1,0:T(8,128)}, u32[]{:S(2)}, u32[]{:S(2)}) collective-permute-start(f32[1536,256]{1,0:T(8,128)} %get-tuple-element.11), channel_id=1, source_target_pairs={{0,8},{2,10},{4,12},{6,14}} | collective-permute-start | bytes 4718600 | tf_op jit(solution)/shard_map/ppermute | solution.py:225
  62.9 16.3 %copy-start.5 = (f32[256,768]{1,0:T(8,128)}, f32[256,768]{1,0:T(8,128)S(1)}, u32[]{:S(2)}) copy-start(f32[256,768]{1,0:T(8,128)S(1)} %collective-permute-done.17.refs_7_) | copy-start | bytes 2359300
  62.9 16.3 %collective-permute-start.20 = (f32[256,640]{1,0:T(8,128)}, f32[256,640]{1,0:T(8,128)}, u32[]{:S(2)}, u32[]{:S(2)}) collective-permute-start(f32[256,640]{1,0:T(8,128)} %collective-permute-done.18.refs_8_), channel_id=1, source_target_pairs={{4,6},{5,7},{12,14},{13,15},{20,22},{21,23},{28,30},{29,31}} | collective-permute-start | bytes 1966088 | tf_op jit(solution)/shard_map/ppermute | solution.py:225
  75.0 4.1 %copy-start.6 = (f32[256,768]{1,0:T(8,128)}, f32[256,768]{1,0:T(8,128)S(1)}, u32[]{:S(2)}) copy-start(f32[256,768]{1,0:T(8,128)S(1)} %collective-permute-done.16.refs_6_) | copy-start | bytes 2359300
  75.0 16.9 %collective-permute-start.19 = (f32[256,640]{1,0:T(8,128)}, f32[256,640]{1,0:T(8,128)}, u32[]{:S(2)}, u32[]{:S(2)}) collective-permute-start(f32[256,640]{1,0:T(8,128)} %collective-permute-done.18.refs_8_), channel_id=1, source_target_pairs={{4,2},{5,3},{12,10},{13,11},{20,18},{21,19},{28,26},{29,27}} | collective-permute-start | bytes 1966088 | tf_op jit(solution)/shard_map/ppermute | solution.py:225
  78.9 13.7 %copy-start.8 = (f32[256,640]{1,0:T(8,128)S(1)}, f32[256,640]{1,0:T(8,128)}, u32[]{:S(2)}) copy-start(f32[256,640]{1,0:T(8,128)} %copy-done.7) | copy-start | bytes 1966084
  79.2 25.6 %collective-permute-start.2 = (f32[256,256]{1,0:T(8,128)S(1)}, f32[256,256]{1,0:T(8,128)S(1)}, u32[]{:S(2)}, u32[]{:S(2)}) collective-permute-start(f32[256,256]{1,0:T(8,128)S(1)} %slice_select_fusion), channel_id=1, source_target_pairs={{0,6}} | collective-permute-start | bytes 786440 | tf_op jit(solution)/shard_map/ppermute | solution.py:225
  92.0 9.9 %collective-permute-start.22 = (f32[256,768]{1,0:T(8,128)S(1)}, f32[256,768]{1,0:T(8,128)S(1)}, u32[]{:S(2)}, u32[]{:S(2)}) collective-permute-start(f32[256,768]{1,0:T(8,128)S(1)} %select_select_fusion), channel_id=1, source_target_pairs={{24,8},{25,9},{26,10},{27,11},{28,12},{29,13},{30,14},{31,15}} | collective-permute-start | bytes 2359304 | tf_op jit(solution)/shard_map/ppermute | solution.py:225
  94.3 10.5 %collective-permute-start.1 = (f32[256,256]{1,0:T(8,128)S(1)}, f32[256,256]{1,0:T(8,128)S(1)}, u32[]{:S(2)}, u32[]{:S(2)}) collective-permute-start(f32[256,256]{1,0:T(8,128)S(1)} %slice_select_fusion), channel_id=1, source_target_pairs={{0,4}} | collective-permute-start | bytes 786440 | tf_op jit(solution)/shard_map/ppermute | solution.py:225
  95.0 4.7 %collective-permute-start.21 = (f32[256,640]{1,0:T(8,128)S(1)}, f32[256,640]{1,0:T(8,128)S(1)}, u32[]{:S(2)}, u32[]{:S(2)}) collective-permute-start(f32[256,640]{1,0:T(8,128)S(1)} %select_select_fusion.2), channel_id=1, source_target_pairs={{24,8},{25,9},{26,10},{27,11},{28,12},{29,13},{30,14},{31,15}} | collective-permute-start | bytes 1966088 | tf_op jit(solution)/shard_map/ppermute | solution.py:225
  95.7 4.7 %collective-permute-start.23 = (f32[256,640]{1,0:T(8,128)S(1)}, f32[256,640]{1,0:T(8,128)S(1)}, u32[]{:S(2)}, u32[]{:S(2)}) collective-permute-start(f32[256,640]{1,0:T(8,128)S(1)} %select_select_fusion.1), channel_id=1, source_target_pairs={{24,8},{25,9},{26,10},{27,11},{28,12},{29,13},{30,14},{31,15}} | collective-permute-start | bytes 1966088 | tf_op jit(solution)/shard_map/ppermute | solution.py:225
  99.7 5.2 %collective-permute-start = (f32[256,256]{1,0:T(8,128)S(1)}, f32[256,256]{1,0:T(8,128)S(1)}, u32[]{:S(2)}, u32[]{:S(2)}) collective-permute-start(f32[256,256]{1,0:T(8,128)S(1)} %slice_select_fusion), channel_id=1, source_target_pairs={{0,2}} | collective-permute-start | bytes 786440 | tf_op jit(solution)/shard_map/ppermute | solution.py:225
  100.5 44.4 %collective-permute-start.10 = (f32[1536,256]{1,0:T(8,128)S(1)}, f32[1536,256]{1,0:T(8,128)}, u32[]{:S(2)}, u32[]{:S(2)}) collective-permute-start(f32[1536,256]{1,0:T(8,128)S(1)} %add_select_fusion), channel_id=1, source_target_pairs={{0,1},{2,3},{4,5},{6,7},{16,17},{18,19},{20,21},{22,23},{8,24},{10... | collective-permute-start | bytes 4718600 | tf_op jit(solution)/shard_map/ppermute | solution.py:225
  101.8 1.7 copy-start.2
  103.5 61.9 %collective-permute-start.27 = (f32[256,2048]{1,0:T(8,128)}, f32[256,2048]{1,0:T(8,128)}, u32[]{:S(2)}, u32[]{:S(2)}) collective-permute-start(f32[256,2048]{1,0:T(8,128)} %pad_maximum_fusion), channel_id=1, source_target_pairs={{8,0},{9,1},{10,2},{11,3},{12,4},{13,5},{14,6},{15,7},{24,16},{25,... | collective-permute-start | bytes 6291464 | tf_op jit(solution)/shard_map/ppermute | solution.py:225
  105.9 0.7 collective-permute-start.3
  106.6 0.7 collective-permute-start.4
  107.4 31.4 %collective-permute-start.5 = (f32[256,256]{1,0:T(8,128)S(1)}, f32[256,256]{1,0:T(8,128)}, u32[]{:S(2)}, u32[]{:S(2)}) collective-permute-start(f32[256,256]{1,0:T(8,128)S(1)} %add.86), channel_id=1, source_target_pairs={{24,16},{26,18},{28,20},{30,22},{1,17},{3,19},{5,21},{7,23}} | collective-permute-start | bytes 786440 | tf_op jit(solution)/shard_map/ppermute | solution.py:225
  139.7 10.1 %collective-permute-start.6 = (f32[256,256]{1,0:T(8,128)S(1)}, f32[256,256]{1,0:T(8,128)}, u32[]{:S(2)}, u32[]{:S(2)}) collective-permute-start(f32[256,256]{1,0:T(8,128)S(1)} %add.87), channel_id=1, source_target_pairs={{1,9},{3,11},{5,13},{7,15},{17,25},{19,27},{21,29},{23,31}} | collective-permute-start | bytes 786440 | tf_op jit(solution)/shard_map/ppermute | solution.py:225
  143.5 8.0 %collective-permute-start.25 = (f32[256,256]{1,0:T(8,128)}, f32[256,256]{1,0:T(8,128)}, u32[]{:S(2)}, u32[]{:S(2)}) collective-permute-start(f32[256,256]{1,0:T(8,128)} %get-tuple-element.13), channel_id=1, source_target_pairs={{8,9},{10,11},{12,13},{14,15},{25,24},{27,26},{29,28},{31,30}} | collective-permute-start | bytes 786440 | tf_op jit(solution)/shard_map/ppermute | solution.py:225
  147.6 23.8 %collective-permute-start.11 = (f32[1536,256]{1,0:T(8,128)}, f32[1536,256]{1,0:T(8,128)}, u32[]{:S(2)}, u32[]{:S(2)}) collective-permute-start(f32[1536,256]{1,0:T(8,128)} %add.91.refs_0_), channel_id=1, source_target_pairs={{0,8},{1,9},{2,10},{3,11},{4,12},{5,13},{6,14},{7,15},{8,0},{9,1},... | collective-permute-start | bytes 4718600 | tf_op jit(solution)/shard_map/ppermute | solution.py:225
  150.8 14.5 %collective-permute-start.24 = (f32[256,256]{1,0:T(8,128)S(1)}, f32[256,256]{1,0:T(8,128)S(1)}, u32[]{:S(2)}, u32[]{:S(2)}) collective-permute-start(f32[256,256]{1,0:T(8,128)S(1)} %get-tuple-element.12), channel_id=1, source_target_pairs={{8,9},{10,11},{12,13},{14,15},{25,24},{27,26},{29,28},{31,30}} | collective-permute-start | bytes 786440 | tf_op jit(solution)/shard_map/ppermute | solution.py:225
  152.5 13.0 %copy-start.3 = (f32[256,640]{1,0:T(8,128)S(1)}, f32[256,640]{1,0:T(8,128)}, u32[]{:S(2)}) copy-start(f32[256,640]{1,0:T(8,128)} %copy-done.2) | copy-start | bytes 1966084
  152.5 12.8 %collective-permute-start.26 = (f32[256,256]{1,0:T(8,128)S(1)}, f32[256,256]{1,0:T(8,128)S(1)}, u32[]{:S(2)}, u32[]{:S(2)}) collective-permute-start(f32[256,256]{1,0:T(8,128)S(1)} %broadcast_select_fusion.1), channel_id=1, source_target_pairs={{8,0},{9,1},{10,2},{11,3},{12,4},{13,5},{14,6},{15,7},{24,16},{25,... | collective-permute-start | bytes 786440 | tf_op jit(solution)/shard_map/ppermute | solution.py:225
  165.3 2.2 %copy-start.1 = (f32[256,256]{1,0:T(8,128)}, f32[256,256]{1,0:T(8,128)S(1)}, u32[]{:S(2)}) copy-start(f32[256,256]{1,0:T(8,128)S(1)} %factor.1.g_ref) | copy-start | bytes 786436
  165.4 2.2 %copy-start = (f32[256,2048]{1,0:T(8,128)S(1)}, f32[256,2048]{1,0:T(8,128)}, u32[]{:S(2)}) copy-start(f32[256,2048]{1,0:T(8,128)} %prior_ref.1) | copy-start | bytes 6291460

commit v2 on v1

--- a/solution.py
+++ b/solution.py
@@ -118,39 +118,43 @@
     return wait
 
 
-def update_kernel(plan, n_p, n_r, a_ref, g_ref, whole_ref, *refs):
-    p_refs = refs[:n_p]
-    r_refs = refs[n_p : n_p + n_r]
-    out_ref, p_buf, r_buf, w_buf, w3_buf, p_sems, r_sems = refs[n_p + n_r :]
+def subtract_product(a_ref, g_ref, p_buf, w3_ref, out_ref):
+    step = pl.program_id(0)
+    tile, cols = a_ref.shape
+    lower = dot3(p_buf[pl.ds(step * tile, tile), :], g_ref[...], (((1,), (1,)), ((), ())))
+    high, low = split(lower)
+    parts = jnp.concatenate([high, high, low], axis=1)
+    width = min(512, cols)
+    for c in range(0, cols, width):
+        out_ref[:, c : c + width] = a_ref[:, c : c + width] - jnp.dot(
+            parts, w3_ref[:, c : c + width], preferred_element_type=jnp.float32
+        )
+    return lower
+
+
+def top_kernel(plan, n_r, a_ref, g_ref, whole_ref, part_ref, rest_ref, *refs):
+    r_refs = refs[:n_r]
+    out_ref, w3_ref, p_buf, r_buf, w_buf, p_sems, r_sems = refs[n_r:]
     step = pl.program_id(0)
     group, row, col = (lax.axis_index(a) for a in AXES)
-    tile = a_ref.shape[0]
+    even = lax.rem(group, 2) == 0
 
     @pl.when(step == 0)
     def _():
-        p_plan, r_plan = plan(group, row, col, whole_ref, p_refs, r_refs, p_buf, r_buf)
-        wait_r = copy_in(r_plan, r_sems)
-        wait_p = copy_in(p_plan, p_sems)
+        wait_r = copy_in(plan(row, whole_ref, r_refs, r_buf), r_sems)
+        wait_p = copy_in([(even, part_ref, p_buf), (~even, rest_ref, p_buf)], p_sems)
         wait_r()
         w = dot3(g_ref[...], r_buf[...])
         w_buf[...] = w
         high, low = split(w)
-        w3_buf[0:B, :] = high
-        w3_buf[B : 2 * B, :] = low
-        w3_buf[2 * B :, :] = high
+        w3_ref[0:B, :] = high
+        w3_ref[B : 2 * B, :] = low
+        w3_ref[2 * B :, :] = high
         wait_p()
 
-    lower = dot3(p_buf[pl.ds(step * tile, tile), :], g_ref[...], (((1,), (1,)), ((), ())))
-    high, low = split(lower)
-    parts = jnp.concatenate([high, high, low], axis=1)
-    cols = a_ref.shape[1]
-    step_cols = min(512, cols)
-    for c in range(0, cols, step_cols):
-        out_ref[:, c : c + step_cols] = a_ref[:, c : c + step_cols] - jnp.dot(
-            parts, w3_buf[:, c : c + step_cols], preferred_element_type=jnp.float32
-        )
-
-    @pl.when((row == 0) & (step * tile < B))
+    lower = subtract_product(a_ref, g_ref, p_buf, w3_ref, out_ref)
+
+    @pl.when((row == 0) & (step == 0))
     def _():
         out_ref[0:B, :] = w_buf[...]
 
@@ -159,37 +163,73 @@
         out_ref[:, 0:B] = lower
 
 
-def update(plan, sizes, a, g, p_list, r_list):
+def bottom_kernel(a_ref, g_ref, w3_ref, part_ref, rest_ref, prev_ref, out_ref, p_buf, p_sems):
+    group, col = lax.axis_index(AXES[0]), lax.axis_index(AXES[2])
+    even = lax.rem(group, 2) == 0
+
+    @pl.when(pl.program_id(0) == 0)
+    def _():
+        copy_in([(even, rest_ref, p_buf), (~even, part_ref, p_buf)], p_sems)()
+
+    lower = subtract_product(a_ref, g_ref, p_buf, w3_ref, out_ref)
+
+    @pl.when((group == 0) & (col == 0))
+    def _():
+        out_ref[:, 0:B] = lower
+
+
+def update_specs(a):
     rows, cols = a.shape
-    tile = 2 * B if rows % (2 * B) == 0 else B
-    any_spec = pl.BlockSpec(memory_space=pl.ANY)
-    n_p, n_r = len(p_list), len(r_list)
-    n_pp, n_rp = sizes
+    half = rows // 2
+    tile = 2 * B if half % (2 * B) == 0 else B
+    params = dict(
+        grid=(half // tile,),
+        compiler_params=pltpu.CompilerParams(vmem_limit_bytes=62 << 20),
+        cost_estimate=pl.CostEstimate(
+            flops=3 * rows * cols * B, bytes_accessed=4 * rows * cols, transcendentals=0
+        ),
+    )
+    fixed = lambda shape: pl.BlockSpec(shape, lambda i: (0, 0))
+    rows_from = lambda first: pl.BlockSpec((tile, cols), lambda i: (i + first // tile, 0))
+    return half, params, fixed, rows_from, pl.BlockSpec(memory_space=pl.ANY)
+
+
+def update_top(plan, n_copies, a, g, part, rest, r_list):
+    rows, cols = a.shape
+    half, params, fixed, rows_from, anywhere = update_specs(a)
     return pl.pallas_call(
-        functools.partial(update_kernel, plan, n_p, n_r),
-        grid=(rows // tile,),
-        in_specs=[
-            pl.BlockSpec((tile, cols), lambda i: (i, 0)),
-            pl.BlockSpec((B, B), lambda i: (0, 0)),
-            any_spec,
-        ]
-        + [any_spec] * (n_p + n_r),
-        out_specs=pl.BlockSpec((tile, cols), lambda i: (i, 0)),
-        out_shape=jax.ShapeDtypeStruct((rows, cols), jnp.float32),
+        functools.partial(top_kernel, plan, len(r_list)),
+        in_specs=[rows_from(0), fixed((B, B))] + [anywhere] * (3 + len(r_list)),
+        out_specs=[rows_from(0), fixed((3 * B, cols))],
+        out_shape=[
+            jax.ShapeDtypeStruct((rows, cols), jnp.float32),
+            jax.ShapeDtypeStruct((3 * B, cols), jnp.bfloat16),
+        ],
         scratch_shapes=[
-            pltpu.VMEM((rows, B), jnp.float32),
+            pltpu.VMEM((half, B), jnp.float32),
             pltpu.VMEM((B, cols), jnp.float32),
             pltpu.VMEM((B, cols), jnp.float32),
-            pltpu.VMEM((3 * B, cols), jnp.bfloat16),
-            pltpu.SemaphoreType.DMA((n_pp,)),
-            pltpu.SemaphoreType.DMA((n_rp,)),
+            pltpu.SemaphoreType.DMA((2,)),
+            pltpu.SemaphoreType.DMA((n_copies,)),
         ],
-        compiler_params=pltpu.CompilerParams(vmem_limit_bytes=62 << 20),
-        cost_estimate=pl.CostEstimate(
-            flops=6 * rows * cols * B, bytes_accessed=8 * rows * cols, transcendentals=0
-        ),
-        name="update",
-    )(a, g, a, *p_list, *r_list)
+        name="top",
+        **params,
+    )(a, g, a, part, rest, *r_list)
+
+
+def update_bottom(a, g, w3, part, rest, prev):
+    rows, cols = a.shape
+    half, params, fixed, rows_from, anywhere = update_specs(a)
+    return pl.pallas_call(
+        bottom_kernel,
+        in_specs=[rows_from(half), fixed((B, B)), fixed((3 * B, cols))] + [anywhere] * 3,
+        out_specs=rows_from(half),
+        out_shape=jax.ShapeDtypeStruct((rows, cols), jnp.float32),
+        input_output_aliases={5: 0},
+        scratch_shapes=[pltpu.VMEM((half, B), jnp.float32), pltpu.SemaphoreType.DMA((2,))],
+        name="bottom",
+        **params,
+    )(a, g, w3, part, rest, prev)
 
 
 def posterior_kernel(prior_ref, g_ref, win_ref, x_ref, out_ref):
@@ -306,21 +346,14 @@
             got = got + send(got, [((last, r, c), (to, r, c)) for r in all_r for c in all_c])
         xs.append(got)
 
-    def plan(group, row, col, whole, p_refs, r_refs, p_buf, r_buf):
-        even = lax.rem(group, 2) == 0
-        top, bottom = p_buf.at[:half, :], p_buf.at[half:, :]
-        p_plan = [
-            (even, p_refs[0], top),
-            (even, p_refs[1], bottom),
-            (~even, p_refs[1], top),
-            (~even, p_refs[0], bottom),
-        ]
-        r_plan = [(row == 0, whole.at[0:B, :], r_buf)]
+    def plan(row, whole, r_refs, r_buf):
+        out = [(row == 0, whole.at[0:B, :], r_buf)]
         for (s, w, r), ref in zip(r_keys, r_refs):
-            r_plan.append((row == r, ref, r_buf.at[:, s : s + w]))
-        return p_plan, r_plan
-
-    block = update(plan, (4, 1 + len(r_keys)), a, g, [part, rest], r_list)
+            out.append((row == r, ref, r_buf.at[:, s : s + w]))
+        return out
+
+    block, w3 = update_top(plan, 1 + len(r_keys), a, g, part, rest, r_list)
+    block = update_bottom(a, g, w3, part, rest, block)
 
     width = prior.shape[0]
     x = jnp.concatenate(xs, axis=1)

time: 200 us -> 203 us (1.015)
  the two profiles are of different devices: /device:TPU:14 before, /device:TPU:11 now
where the time goes in v2:
time: 203 us; the launch traced here: 202 us
  waiting for transfers between devices  95.1 us (47%)
  Pallas kernels  49.3 us (24%)
  starting transfers between devices  34.1 us (17%)
  other arithmetic  13.5 us (7%)
  local copies, waits for them, and re-layouts  8.7 us (4%)
    ppermute x28, waiting for transfers between devices, send(): return lax.ppermute(x, AXES, [(ident(*s), ident(*d)) for s, d in pairs])  95.1 us
    ppermute x28, starting transfers between devices, send(): return lax.ppermute(x, AXES, [(ident(*s), ident(*d)) for s, d in pairs])  34.1 us
    pallas_call x1, Pallas kernels, update_top(): pl.pallas_call(functools.partial(top_kernel, plan, len(r_list)), in_specs...  17.9 us
    pallas_call x1, Pallas kernels, update_bottom(): pl.pallas_call(bottom_kernel, in_specs=[rows_from(half), fixed((B, B)), f...  16.4 us
    pallas_call x1, Pallas kernels, inverse_factor(): pl.pallas_call(factor_kernel, out_shape=jax.ShapeDtypeStruct((n, n), jnp....  11.2 us
  transfers between devices with their start and end apart: 28, of which 8 were waited for; matrix products, arithmetic and copies ran while one was open for 9% of the time, Pallas kernels for 7%

profile of v2, /device:TPU:11, one launch (start us, length us, event | category | flops | bytes accessed | tf_op | source)
XLA Modules:
  0.0 202.2 jit_solution(7891973189551848647)
XLA Ops:
  0.6 1.2 slice.28
  1.8 1.4 fusion
  3.2 0.7 collective-permute-start.15
  3.9 0.7 collective-permute-start.12
  4.6 0.7 collective-permute-start.18
  5.4 0.7 collective-permute-start.14
  6.1 1.3 collective-permute-start.13
  7.4 0.7 collective-permute-start.17
  8.1 1.3 collective-permute-start.16
  9.4 3.8 %fusion.1 = (f32[1536,256]{1,0:T(8,128)}, f32[1536,256]{1,0:T(8,128)}) fusion(f32[3072,2048]{1,0:T(8,128)} %bitcast.4), kind=kLoop, calls=%fused_computation.13 | loop fusion | bytes 6291456 | tf_op jit(solution)/shard_map/slice | solution.py:312
  13.2 1.9 collective-permute-start.8
  15.1 1.8 collective-permute-start.9
  16.9 37.9 %collective-permute-done.13.refs_1_ = f32[256,640]{1,0:T(8,128)S(1)} collective-permute-done((f32[256,640]{1,0:T(8,128)S(1)}, f32[256,640]{1,0:T(8,128)S(1)}, u32[]{:S(2)}, u32[]{:S(2)}) %collective-permute-start.13) | collective-permute-done | bytes 655392 | tf_op jit(solution)/shard_map/ppermute | solution.py:265
  54.8 1.9 collective-permute-start.7
  56.7 1.5 collective-permute-start.20
  58.2 13.5 %collective-permute-done.16.refs_4_ = f32[256,768]{1,0:T(8,128)S(1)} collective-permute-done((f32[256,768]{1,0:T(8,128)S(1)}, f32[256,768]{1,0:T(8,128)S(1)}, u32[]{:S(2)}, u32[]{:S(2)}) %collective-permute-start.16) | collective-permute-done | bytes 786464 | tf_op jit(solution)/shard_map/ppermute | solution.py:265
  71.7 1.3 collective-permute-start.19
  73.0 1.0 slice_select_fusion
  74.0 1.6 select_select_fusion.2
  75.8 0.8 collective-permute-start.2
  76.7 11.1 %collective-permute-done.19.refs_7_ = f32[256,640]{1,0:T(8,128)} collective-permute-done((f32[256,640]{1,0:T(8,128)}, f32[256,640]{1,0:T(8,128)}, u32[]{:S(2)}, u32[]{:S(2)}) %collective-permute-start.19) | collective-permute-done | bytes 655392 | tf_op jit(solution)/shard_map/ppermute | solution.py:265
  87.7 2.2 %collective-permute-start.22 = (f32[256,768]{1,0:T(8,128)S(1)}, f32[256,768]{1,0:T(8,128)S(1)}, u32[]{:S(2)}, u32[]{:S(2)}) collective-permute-start(f32[256,768]{1,0:T(8,128)S(1)} %select_select_fusion), channel_id=1, source_target_pairs={{24,8},{25,9},{26,10},{27,11},{28,12},{29,13},{30,14},{31,15}} | collective-permute-start | bytes 2359304 | tf_op jit(solution)/shard_map/ppermute | solution.py:265
  90.0 1.5 select_select_fusion.1
  92.2 1.3 collective-permute-start.21
  93.5 1.3 collective-permute-start.23
  94.8 3.2 %add_select_fusion = f32[1536,256]{1,0:T(8,128)S(1)} fusion(f32[1536,256]{1,0:T(8,128)} %collective-permute-done.9, f32[1536,256]{1,0:T(8,128)} %collective-permute-done.7, f32[1536,256]{1,0:T(8,128)} %collective-permute-done.8, pred[]{:T(512)S(6)} %and.30, f32[3072,2048]{1,0:T(8,128)} %bitcast.6), kind=kLoop, calls=%fused_computation.1 | loop fusion | flops 1179648 | bytes 7864321 | tf_op jit(solution)/shard_map/jit(_where)/select_n | solution.py:320
  98.1 7.7 %collective-permute-done.21 = f32[256,640]{1,0:T(8,128)S(1)} collective-permute-done((f32[256,640]{1,0:T(8,128)S(1)}, f32[256,640]{1,0:T(8,128)S(1)}, u32[]{:S(2)}, u32[]{:S(2)}) %collective-permute-start.21) | collective-permute-done | bytes 655392 | tf_op jit(solution)/shard_map/ppermute | solution.py:265
  106.6 6.3 %collective-permute-done.23 = f32[256,640]{1,0:T(8,128)S(1)} collective-permute-done((f32[256,640]{1,0:T(8,128)S(1)}, f32[256,640]{1,0:T(8,128)S(1)}, u32[]{:S(2)}, u32[]{:S(2)}) %collective-permute-start.23) | collective-permute-done | bytes 655392 | tf_op jit(solution)/shard_map/ppermute | solution.py:265
  112.9 1.3 collective-permute-start.10
  114.4 1.6 pad_maximum_fusion
  116.0 2.7 %collective-permute-start.27 = (f32[256,2048]{1,0:T(8,128)}, f32[256,2048]{1,0:T(8,128)}, u32[]{:S(2)}, u32[]{:S(2)}) collective-permute-start(f32[256,2048]{1,0:T(8,128)} %pad_maximum_fusion), channel_id=1, source_target_pairs={{8,0},{9,1},{10,2},{11,3},{12,4},{13,5},{14,6},{15,7},{24,16},{25,... | collective-permute-start | bytes 6291464 | tf_op jit(solution)/shard_map/ppermute | solution.py:265
  118.6 1.0 add_add_fusion
  120.4 1.3 collective-permute-start.4
  121.7 15.1 %collective-permute-done.4 = f32[256,256]{1,0:T(8,128)S(1)} collective-permute-done((f32[256,256]{1,0:T(8,128)S(1)}, f32[256,256]{1,0:T(8,128)S(1)}, u32[]{:S(2)}, u32[]{:S(2)}) %collective-permute-start.4) | collective-permute-done | bytes 262176 | tf_op jit(solution)/shard_map/ppermute | solution.py:265
  136.8 1.3 collective-permute-start.5
  138.2 1.1 collective-permute-done.5
  140.0 1.1 constant_dynamic-slice_fusion.1
  141.1 1.3 collective-permute-start.25
  142.4 1.6 add.91.part_ref
  144.6 1.3 collective-permute-start.24
  145.9 2.4 %collective-permute-done.25 = f32[256,256]{1,0:T(8,128)} collective-permute-done((f32[256,256]{1,0:T(8,128)S(1)}, f32[256,256]{1,0:T(8,128)}, u32[]{:S(2)}, u32[]{:S(2)}) %collective-permute-start.25) | collective-permute-done | bytes 262176 | tf_op jit(solution)/shard_map/ppermute | solution.py:265
  148.3 1.0 broadcast_select_fusion.1
  149.3 1.6 collective-permute-start.26
  150.9 11.2 %factor.1.g_ref = f32[256,256]{1,0:T(8,128)S(1)} custom-call(f32[256,256]{1,0:T(8,128)S(1)} %add.88.d_ref), custom_call_target="tpu_custom_call" | custom-call | flops 4000000000 | bytes 1048576 | tf_op jit(solution)/shard_map/factor/pallas_call | solution.py:99
  162.9 1.0 copy-done.1
  163.9 3.8 %posterior.1 = f32[256,2048]{1,0:T(8,128)} custom-call(f32[256,2048]{1,0:T(8,128)S(1)} %copy-done.1, f32[256,256]{1,0:T(8,128)S(1)} %factor.1.g_ref, f32[256,256]{1,0:T(8,128)S(1)} %select_select_fusion.3.win_ref, f32[256,2048]{1,0:T(8,128)S(1)} %broadcast_select_fusion.x_ref), custom_call_target="tpu_custom_call" | custom-call | flops 805306368 | bytes 3145728 | tf_op jit(solution)/shard_map/posterior/pallas_call | solution.py:243
  167.7 17.9 %top.1 = (f32[3072,2048]{1,0:T(8,128)}, bf16[768,2048]{1,0:T(8,128)(2,1)}) custom-call(f32[3072,2048]{1,0:T(8,128)} %bitcast.8, f32[256,256]{1,0:T(8,128)} %copy-done, f32[3072,2048]{1,0:T(8,128)} %bitcast.9, f32[1536,256]{1,0:T(8,128)} %copy-done.2, f32[1536,256]{1,0:T(8,128)} %collective-permute-done.11.rest_ref, f32[256,640]{1,0:T(8,128)} %copy-done.12, ...), custom_call_target="tpu_custom_call" | custom-call | flops 4831838208 | bytes 25165824 | tf_op jit(solution)/shard_map/top/pallas_call | solution.py:200
  185.6 16.4 %bottom.1 = f32[3072,2048]{1,0:T(8,128)} custom-call(f32[3072,2048]{1,0:T(8,128)} %bitcast.10, f32[256,256]{1,0:T(8,128)} %copy-done, bf16[768,2048]{1,0:T(8,128)(2,1)} %get-tuple-element.10.w3_ref, f32[1536,256]{1,0:T(8,128)} %copy-done.2, f32[1536,256]{1,0:T(8,128)} %collective-permute-done.11.rest_ref, ...), custom_call_target="tpu_custom_call", output_to_operand_aliasing={{}: (5, {})} | custom-call | flops 4831838208 | bytes 25165824 | tf_op jit(solution)/shard_map/bottom/pallas_call | solution.py:223
  (74 shorter events, 4.5 us)
Async XLA Ops:
  3.2 2.2 %copy-start.19 = (f32[256,640]{1,0:T(8,128)}, f32[256,640]{1,0:T(8,128)S(1)}, u32[]{:S(2)}) copy-start(f32[256,640]{1,0:T(8,128)S(1)} %get-tuple-element.7) | copy-start | bytes 1966084
  3.2 10.0 %copy-start.17 = (f32[256,640]{1,0:T(8,128)}, f32[256,640]{1,0:T(8,128)S(1)}, u32[]{:S(2)}) copy-start(f32[256,640]{1,0:T(8,128)S(1)} %get-tuple-element.9) | copy-start | bytes 1966084
  3.2 4.2 %collective-permute-start.15 = (f32[256,768]{1,0:T(8,128)S(1)}, f32[256,768]{1,0:T(8,128)S(1)}, u32[]{:S(2)}, u32[]{:S(2)}) collective-permute-start(f32[256,768]{1,0:T(8,128)S(1)} %slice.28), channel_id=1, source_target_pairs={{0,4},{1,5},{8,12},{9,13},{16,20},{17,21},{24,28},{25,29}} | collective-permute-start | bytes 2359304 | tf_op jit(solution)/shard_map/ppermute | solution.py:265
  3.9 1.4 collective-permute-start.12
  4.6 8.6 %collective-permute-start.18 = (f32[256,640]{1,0:T(8,128)S(1)}, f32[256,640]{1,0:T(8,128)S(1)}, u32[]{:S(2)}, u32[]{:S(2)}) collective-permute-start(f32[256,640]{1,0:T(8,128)S(1)} %get-tuple-element.9), channel_id=1, source_target_pairs={{0,4},{1,5},{8,12},{9,13},{16,20},{17,21},{24,28},{25,29}} | collective-permute-start | bytes 1966088 | tf_op jit(solution)/shard_map/ppermute | solution.py:265
  5.4 7.8 %copy-start.12 = (f32[256,640]{1,0:T(8,128)}, f32[256,640]{1,0:T(8,128)S(1)}, u32[]{:S(2)}) copy-start(f32[256,640]{1,0:T(8,128)S(1)} %collective-permute-done.12.refs_0_) | copy-start | bytes 1966084
  5.4 9.7 %collective-permute-start.14 = (f32[256,640]{1,0:T(8,128)S(1)}, f32[256,640]{1,0:T(8,128)S(1)}, u32[]{:S(2)}, u32[]{:S(2)}) collective-permute-start(f32[256,640]{1,0:T(8,128)S(1)} %collective-permute-done.12.refs_0_), channel_id=1, source_target_pairs={{4,6},{5,7},{12,14},{13,15},{20,22},{21,23},{28,30},{29,31}} | collective-permute-start | bytes 1966088 | tf_op jit(solution)/shard_map/ppermute | solution.py:265
  6.1 48.7 %collective-permute-start.13 = (f32[256,640]{1,0:T(8,128)S(1)}, f32[256,640]{1,0:T(8,128)S(1)}, u32[]{:S(2)}, u32[]{:S(2)}) collective-permute-start(f32[256,640]{1,0:T(8,128)S(1)} %collective-permute-done.12.refs_0_), channel_id=1, source_target_pairs={{4,2},{5,3},{12,10},{13,11},{20,18},{21,19},{28,26},{29,27}} | collective-permute-start | bytes 1966088 | tf_op jit(solution)/shard_map/ppermute | solution.py:265
  7.4 68.2 %copy-start.9 = (f32[256,768]{1,0:T(8,128)}, f32[256,768]{1,0:T(8,128)S(1)}, u32[]{:S(2)}) copy-start(f32[256,768]{1,0:T(8,128)S(1)} %collective-permute-done.15.refs_3_) | copy-start | bytes 2359300
  7.4 49.3 %collective-permute-start.17 = (f32[256,768]{1,0:T(8,128)S(1)}, f32[256,768]{1,0:T(8,128)S(1)}, u32[]{:S(2)}, u32[]{:S(2)}) collective-permute-start(f32[256,768]{1,0:T(8,128)S(1)} %collective-permute-done.15.refs_3_), channel_id=1, source_target_pairs={{4,6},{5,7},{12,14},{13,15},{20,22},{21,23},{28,30},{29,31}} | collective-permute-start | bytes 2359304 | tf_op jit(solution)/shard_map/ppermute | solution.py:265
  8.1 63.5 %collective-permute-start.16 = (f32[256,768]{1,0:T(8,128)S(1)}, f32[256,768]{1,0:T(8,128)S(1)}, u32[]{:S(2)}, u32[]{:S(2)}) collective-permute-start(f32[256,768]{1,0:T(8,128)S(1)} %collective-permute-done.15.refs_3_), channel_id=1, source_target_pairs={{4,2},{5,3},{12,10},{13,11},{20,18},{21,19},{28,26},{29,27}} | collective-permute-start | bytes 2359304 | tf_op jit(solution)/shard_map/ppermute | solution.py:265
  13.2 41.6 %copy-start.13 = (f32[256,640]{1,0:T(8,128)}, f32[256,640]{1,0:T(8,128)S(1)}, u32[]{:S(2)}) copy-start(f32[256,640]{1,0:T(8,128)S(1)} %collective-permute-done.18.refs_6_) | copy-start | bytes 1966084
  13.2 78.2 %collective-permute-start.8 = (f32[1536,256]{1,0:T(8,128)}, f32[1536,256]{1,0:T(8,128)}, u32[]{:S(2)}, u32[]{:S(2)}) collective-permute-start(f32[1536,256]{1,0:T(8,128)} %get-tuple-element.14), channel_id=1, source_target_pairs={{0,16},{2,18},{4,20},{6,22}} | collective-permute-start | bytes 4718600 | tf_op jit(solution)/shard_map/ppermute | solution.py:265
  15.1 41.6 %copy-start.15 = (f32[256,640]{1,0:T(8,128)}, f32[256,640]{1,0:T(8,128)S(1)}, u32[]{:S(2)}) copy-start(f32[256,640]{1,0:T(8,128)S(1)} %collective-permute-done.14.refs_2_) | copy-start | bytes 1966084
  15.1 77.0 %collective-permute-start.9 = (f32[1536,256]{1,0:T(8,128)}, f32[1536,256]{1,0:T(8,128)}, u32[]{:S(2)}, u32[]{:S(2)}) collective-permute-start(f32[1536,256]{1,0:T(8,128)} %get-tuple-element.15), channel_id=1, source_target_pairs={{0,9},{2,11},{4,13},{6,15}} | collective-permute-start | bytes 4718600 | tf_op jit(solution)/shard_map/ppermute | solution.py:265
  54.8 1.9 copy-start.16
  54.8 38.7 %collective-permute-start.7 = (f32[1536,256]{1,0:T(8,128)}, f32[1536,256]{1,0:T(8,128)}, u32[]{:S(2)}, u32[]{:S(2)}) collective-permute-start(f32[1536,256]{1,0:T(8,128)} %get-tuple-element.15), channel_id=1, source_target_pairs={{0,8},{2,10},{4,12},{6,14}} | collective-permute-start | bytes 4718600 | tf_op jit(solution)/shard_map/ppermute | solution.py:265
  56.7 19.1 %copy-start.10 = (f32[256,768]{1,0:T(8,128)}, f32[256,768]{1,0:T(8,128)S(1)}, u32[]{:S(2)}) copy-start(f32[256,768]{1,0:T(8,128)S(1)} %collective-permute-done.17.refs_5_) | copy-start | bytes 2359300
  56.7 19.1 %collective-permute-start.20 = (f32[256,640]{1,0:T(8,128)}, f32[256,640]{1,0:T(8,128)}, u32[]{:S(2)}, u32[]{:S(2)}) collective-permute-start(f32[256,640]{1,0:T(8,128)} %copy-done.13), channel_id=1, source_target_pairs={{4,6},{5,7},{12,14},{13,15},{20,22},{21,23},{28,30},{29,31}} | collective-permute-start | bytes 1966088 | tf_op jit(solution)/shard_map/ppermute | solution.py:265
  71.7 4.1 %copy-start.11 = (f32[256,768]{1,0:T(8,128)}, f32[256,768]{1,0:T(8,128)S(1)}, u32[]{:S(2)}) copy-start(f32[256,768]{1,0:T(8,128)S(1)} %collective-permute-done.16.refs_4_) | copy-start | bytes 2359300
  71.7 16.0 %collective-permute-start.19 = (f32[256,640]{1,0:T(8,128)}, f32[256,640]{1,0:T(8,128)}, u32[]{:S(2)}, u32[]{:S(2)}) collective-permute-start(f32[256,640]{1,0:T(8,128)} %copy-done.13), channel_id=1, source_target_pairs={{4,2},{5,3},{12,10},{13,11},{20,18},{21,19},{28,26},{29,27}} | collective-permute-start | bytes 1966088 | tf_op jit(solution)/shard_map/ppermute | solution.py:265
  75.6 14.3 %copy-start.14 = (f32[256,640]{1,0:T(8,128)S(1)}, f32[256,640]{1,0:T(8,128)}, u32[]{:S(2)}) copy-start(f32[256,640]{1,0:T(8,128)} %copy-done.13) | copy-start | bytes 1966084
  75.6 14.3 %copy-start.18 = (f32[256,640]{1,0:T(8,128)S(1)}, f32[256,640]{1,0:T(8,128)}, u32[]{:S(2)}) copy-start(f32[256,640]{1,0:T(8,128)} %copy-done.17) | copy-start | bytes 1966084
  75.8 42.8 %collective-permute-start.2 = (f32[256,256]{1,0:T(8,128)S(1)}, f32[256,256]{1,0:T(8,128)S(1)}, u32[]{:S(2)}, u32[]{:S(2)}) collective-permute-start(f32[256,256]{1,0:T(8,128)S(1)} %slice_select_fusion), channel_id=1, source_target_pairs={{0,6}} | collective-permute-start | bytes 786440 | tf_op jit(solution)/shard_map/ppermute | solution.py:265
  87.7 26.5 %collective-permute-start.22 = (f32[256,768]{1,0:T(8,128)S(1)}, f32[256,768]{1,0:T(8,128)S(1)}, u32[]{:S(2)}, u32[]{:S(2)}) collective-permute-start(f32[256,768]{1,0:T(8,128)S(1)} %select_select_fusion), channel_id=1, source_target_pairs={{24,8},{25,9},{26,10},{27,11},{28,12},{29,13},{30,14},{31,15}} | collective-permute-start | bytes 2359304 | tf_op jit(solution)/shard_map/ppermute | solution.py:265
  91.5 27.2 %collective-permute-start.1 = (f32[256,256]{1,0:T(8,128)S(1)}, f32[256,256]{1,0:T(8,128)S(1)}, u32[]{:S(2)}, u32[]{:S(2)}) collective-permute-start(f32[256,256]{1,0:T(8,128)S(1)} %slice_select_fusion), channel_id=1, source_target_pairs={{0,4}} | collective-permute-start | bytes 786440 | tf_op jit(solution)/shard_map/ppermute | solution.py:265
  92.2 13.7 %collective-permute-start.21 = (f32[256,640]{1,0:T(8,128)S(1)}, f32[256,640]{1,0:T(8,128)S(1)}, u32[]{:S(2)}, u32[]{:S(2)}) collective-permute-start(f32[256,640]{1,0:T(8,128)S(1)} %select_select_fusion.2), channel_id=1, source_target_pairs={{24,8},{25,9},{26,10},{27,11},{28,12},{29,13},{30,14},{31,15}} | collective-permute-start | bytes 1966088 | tf_op jit(solution)/shard_map/ppermute | solution.py:265
  93.5 19.4 %collective-permute-start.23 = (f32[256,640]{1,0:T(8,128)S(1)}, f32[256,640]{1,0:T(8,128)S(1)}, u32[]{:S(2)}, u32[]{:S(2)}) collective-permute-start(f32[256,640]{1,0:T(8,128)S(1)} %select_select_fusion.1), channel_id=1, source_target_pairs={{24,8},{25,9},{26,10},{27,11},{28,12},{29,13},{30,14},{31,15}} | collective-permute-start | bytes 1966088 | tf_op jit(solution)/shard_map/ppermute | solution.py:265
  98.1 16.3 %copy-start.3 = (f32[1536,256]{1,0:T(8,128)}, f32[1536,256]{1,0:T(8,128)S(1)}, u32[]{:S(2)}) copy-start(f32[1536,256]{1,0:T(8,128)S(1)} %add_select_fusion) | copy-start | bytes 4718596
  105.8 12.8 %collective-permute-start = (f32[256,256]{1,0:T(8,128)S(1)}, f32[256,256]{1,0:T(8,128)S(1)}, u32[]{:S(2)}, u32[]{:S(2)}) collective-permute-start(f32[256,256]{1,0:T(8,128)S(1)} %slice_select_fusion), channel_id=1, source_target_pairs={{0,2}} | collective-permute-start | bytes 786440 | tf_op jit(solution)/shard_map/ppermute | solution.py:265
  106.6 7.8 %copy-start.5 = (f32[256,640]{1,0:T(8,128)}, f32[256,640]{1,0:T(8,128)S(1)}, u32[]{:S(2)}) copy-start(f32[256,640]{1,0:T(8,128)S(1)} %add.96) | copy-start | bytes 1966084
  112.9 29.5 %collective-permute-start.10 = (f32[1536,256]{1,0:T(8,128)S(1)}, f32[1536,256]{1,0:T(8,128)}, u32[]{:S(2)}, u32[]{:S(2)}) collective-permute-start(f32[1536,256]{1,0:T(8,128)S(1)} %add_select_fusion), channel_id=1, source_target_pairs={{0,1},{2,3},{4,5},{6,7},{16,17},{18,19},{20,21},{22,23},{8,24},{10... | collective-permute-start | bytes 4718600 | tf_op jit(solution)/shard_map/ppermute | solution.py:265
  114.2 1.7 copy-start.7
  116.0 46.3 %collective-permute-start.27 = (f32[256,2048]{1,0:T(8,128)}, f32[256,2048]{1,0:T(8,128)}, u32[]{:S(2)}, u32[]{:S(2)}) collective-permute-start(f32[256,2048]{1,0:T(8,128)} %pad_maximum_fusion), channel_id=1, source_target_pairs={{8,0},{9,1},{10,2},{11,3},{12,4},{13,5},{14,6},{15,7},{24,16},{25,... | collective-permute-start | bytes 6291464 | tf_op jit(solution)/shard_map/ppermute | solution.py:265
  119.7 0.7 collective-permute-start.3
  120.4 16.4 %collective-permute-start.4 = (f32[256,256]{1,0:T(8,128)S(1)}, f32[256,256]{1,0:T(8,128)S(1)}, u32[]{:S(2)}, u32[]{:S(2)}) collective-permute-start(f32[256,256]{1,0:T(8,128)S(1)} %add.85), channel_id=1, source_target_pairs={{0,1},{2,3},{4,5},{6,7},{8,24},{10,26},{12,28},{14,30}} | collective-permute-start | bytes 786440 | tf_op jit(solution)/shard_map/ppermute | solution.py:265
  136.8 2.4 %collective-permute-start.5 = (f32[256,256]{1,0:T(8,128)S(1)}, f32[256,256]{1,0:T(8,128)S(1)}, u32[]{:S(2)}, u32[]{:S(2)}) collective-permute-start(f32[256,256]{1,0:T(8,128)S(1)} %add.86), channel_id=1, source_target_pairs={{24,16},{26,18},{28,20},{30,22},{1,17},{3,19},{5,21},{7,23}} | collective-permute-start | bytes 786440 | tf_op jit(solution)/shard_map/ppermute | solution.py:265
  138.2 4.2 %copy-start.4 = (f32[1536,256]{1,0:T(8,128)S(1)}, f32[1536,256]{1,0:T(8,128)}, u32[]{:S(2)}) copy-start(f32[1536,256]{1,0:T(8,128)} %copy-done.3) | copy-start | bytes 4718596
  139.3 5.2 %collective-permute-start.6 = (f32[256,256]{1,0:T(8,128)S(1)}, f32[256,256]{1,0:T(8,128)S(1)}, u32[]{:S(2)}, u32[]{:S(2)}) collective-permute-start(f32[256,256]{1,0:T(8,128)S(1)} %add.87), channel_id=1, source_target_pairs={{1,9},{3,11},{5,13},{7,15},{17,25},{19,27},{21,29},{23,31}} | collective-permute-start | bytes 786440 | tf_op jit(solution)/shard_map/ppermute | solution.py:265
  141.1 7.2 %collective-permute-start.25 = (f32[256,256]{1,0:T(8,128)S(1)}, f32[256,256]{1,0:T(8,128)}, u32[]{:S(2)}, u32[]{:S(2)}) collective-permute-start(f32[256,256]{1,0:T(8,128)S(1)} %get-tuple-element.17), channel_id=1, source_target_pairs={{8,9},{10,11},{12,13},{14,15},{25,24},{27,26},{29,28},{31,30}} | collective-permute-start | bytes 786440 | tf_op jit(solution)/shard_map/ppermute | solution.py:265
  144.0 18.1 %copy-start.2 = (f32[1536,256]{1,0:T(8,128)}, f32[1536,256]{1,0:T(8,128)S(1)}, u32[]{:S(2)}) copy-start(f32[1536,256]{1,0:T(8,128)S(1)} %add.91.part_ref) | copy-start | bytes 4718596
  144.0 23.7 %collective-permute-start.11 = (f32[1536,256]{1,0:T(8,128)S(1)}, f32[1536,256]{1,0:T(8,128)}, u32[]{:S(2)}, u32[]{:S(2)}) collective-permute-start(f32[1536,256]{1,0:T(8,128)S(1)} %add.91.part_ref), channel_id=1, source_target_pairs={{0,8},{1,9},{2,10},{3,11},{4,12},{5,13},{6,14},{7,15},{8,0},{9,1},... | collective-permute-start | bytes 4718600 | tf_op jit(solution)/shard_map/ppermute | solution.py:265
  144.6 17.6 %collective-permute-start.24 = (f32[256,256]{1,0:T(8,128)S(1)}, f32[256,256]{1,0:T(8,128)S(1)}, u32[]{:S(2)}, u32[]{:S(2)}) collective-permute-start(f32[256,256]{1,0:T(8,128)S(1)} %get-tuple-element.16), channel_id=1, source_target_pairs={{8,9},{10,11},{12,13},{14,15},{25,24},{27,26},{29,28},{31,30}} | collective-permute-start | bytes 786440 | tf_op jit(solution)/shard_map/ppermute | solution.py:265
  149.3 13.0 %copy-start.6 = (f32[256,640]{1,0:T(8,128)S(1)}, f32[256,640]{1,0:T(8,128)}, u32[]{:S(2)}) copy-start(f32[256,640]{1,0:T(8,128)} %copy-done.5) | copy-start | bytes 1966084
  149.3 13.0 %copy-start.8 = (f32[256,640]{1,0:T(8,128)S(1)}, f32[256,640]{1,0:T(8,128)}, u32[]{:S(2)}) copy-start(f32[256,640]{1,0:T(8,128)} %copy-done.7) | copy-start | bytes 1966084
  149.3 12.9 %collective-permute-start.26 = (f32[256,256]{1,0:T(8,128)S(1)}, f32[256,256]{1,0:T(8,128)S(1)}, u32[]{:S(2)}, u32[]{:S(2)}) collective-permute-start(f32[256,256]{1,0:T(8,128)S(1)} %broadcast_select_fusion.1), channel_id=1, source_target_pairs={{8,0},{9,1},{10,2},{11,3},{12,4},{13,5},{14,6},{15,7},{24,16},{25,... | collective-permute-start | bytes 786440 | tf_op jit(solution)/shard_map/ppermute | solution.py:265
  162.2 0.7 copy-start
  162.3 1.6 copy-start.1
